TPU v7x, 128 devices: a whole 4x4x4 slice. The times are simulated.
128 devices in a mesh: dp: 8 (over y, x_lo), tensor: 16 (over x_hi, z, core).
Axes of the slice: x: 4 (x_hi: 2, x_lo: 2; x = x_hi * 2 + x_lo), y: 4, z: 4, core: 2. Of those that a mesh axis runs over, the one named last changes fastest.
Arguments:
- grad_out: bfloat16 [8192, 8192], P(('dp', 'tensor')), may hold values from -24 to 24
- out_weight: bfloat16 [8192, 8192], P('dp', 'tensor'), may hold values from -0.0625 to 0.0625
- query: bfloat16 [8192, 8192], P('dp', 'tensor'), may hold values from -6 to 6, as said below
- keys: bfloat16 [8192, 512], P('dp'), may hold values from -6 to 6
- values: bfloat16 [8192, 512], P('dp'), may hold values from -6 to 6
- attended: bfloat16 [8192, 8192], P('dp', 'tensor'), may hold values from -6 to 6, as said below
- stats: float32 [64, 8192], P('tensor', 'dp'), as said below
Outputs:
- query_grad: bfloat16 [8192, 8192], P('dp', 'tensor')
- key_grad: bfloat16 [8192, 512], P('dp', 'tensor')
- value_grad: bfloat16 [8192, 512], P('dp', 'tensor')
- weight_grad: bfloat16 [8192, 8192], P('dp', 'tensor')
Inputs may be any that keep to these rules, and one draw needn't show every extreme that they name: query, keys and values are independent draws. attended is the causal attention output of the given query, keys and values within each sequence of 1024 rows: query head h uses key head h // 16, scores scaled by 128 ** -0.5, softmax over keys at or before the query. stats[h, t] is the logarithm of the sum of exp(score) over the keys that row t of head h attends to, for the same scores.
All inputs are finite; a program needn't handle non-finite values.
Results may differ from a plain program's by a relative error of at most 0.013.
Values may be sent and summed in bfloat16 or wider, within the bound.
A program may use at most 192 MiB of HBM per device.

v0:
```python
import jax
import jax.numpy as jnp
from jax import lax
from jax.sharding import Mesh
from jax.sharding import PartitionSpec as P

HD = 128
HEAD_DEV = 4
GROUP = 16
DP = ("dp_0", "dp_1")
DP_TENSOR = ("dp_0", "dp_1", "tensor")


def gathered_by_axis(x, axes, dim):
    if not axes:
        return x
    nearer = lax.all_gather(x, axes[-1], axis=dim, tiled=True)
    return gathered_by_axis(nearer, axes[:-1], dim)


def sum_by_axis(terms, axes):
    subtotal = terms.astype(jnp.bfloat16)
    for axis in axes:
        subtotal = lax.psum_scatter(subtotal, axis, scatter_dimension=0, tiled=True)
    return subtotal.astype(jnp.float32)


def partner(value, axis, apart):
    mask = 2**apart
    pairs = [(source, source ^ mask) for source in range(lax.axis_size(axis))]
    return lax.ppermute(value, axis, pairs)


def attention_grads(query, key_one, value_one, attended, grad_att, stats):
    length = query.shape[0]
    score_scale = HD ** (-0.5)
    query_heads = query.reshape(length, HEAD_DEV, HD)
    grad_heads = grad_att.reshape(length, HEAD_DEV, HD)
    attended_heads = attended.reshape(length, HEAD_DEV, HD)
    positions = jnp.arange(length, dtype=jnp.int32)
    causal = positions[:, None] >= positions[None, :]
    scores = (
        jnp.einsum("qgd,kd->gqk", query_heads, key_one, preferred_element_type=jnp.float32)
        * score_scale
    )
    attention = jnp.where(causal[None], jnp.exp(scores - stats[:, :, None]), 0.0)
    attention_low = attention.astype(jnp.bfloat16)
    grad_attention = jnp.einsum(
        "qgd,kd->gqk", grad_heads, value_one, preferred_element_type=jnp.float32
    )
    row_offset = jnp.sum(
        grad_heads.astype(jnp.float32) * attended_heads.astype(jnp.float32), axis=2
    )
    grad_scores = (attention * (grad_attention - row_offset.T[:, :, None])).astype(jnp.bfloat16)
    query_grad = (
        jnp.einsum("gqk,kd->qgd", grad_scores, key_one, preferred_element_type=jnp.float32)
        * score_scale
    )
    query_grad = query_grad.astype(jnp.bfloat16).reshape(length, HEAD_DEV * HD)
    key_part = (
        jnp.einsum("gqk,qgd->kd", grad_scores, query_heads, preferred_element_type=jnp.float32)
        * score_scale
    )
    value_part = jnp.einsum(
        "gqk,qgd->kd", attention_low, grad_heads, preferred_element_type=jnp.float32
    )
    return (query_grad, key_part, value_part)


def per_device(grad_out, out_weight, query, keys, values, attended, stats):
    grad_rows = lax.all_gather(grad_out, "tensor", axis=0, tiled=True)
    grad_block = grad_rows
    grad_att = jnp.dot(
        grad_block, gathered_by_axis(out_weight, DP, 0), preferred_element_type=jnp.float32
    ).astype(jnp.bfloat16)
    grad_block = grad_rows
    weight_grad = sum_by_axis(
        lax.dot_general(
            grad_block, attended, (((0,), (0,)), ((), ())), preferred_element_type=jnp.float32
        ),
        DP,
    ).astype(jnp.bfloat16)
    tensor_index = lax.axis_index("tensor")
    key_head = tensor_index * HEAD_DEV // GROUP
    key_one = lax.dynamic_slice_in_dim(keys, key_head * HD, HD, 1)
    value_one = lax.dynamic_slice_in_dim(values, key_head * HD, HD, 1)
    query_grad, key_part, value_part = attention_grads(
        query, key_one, value_one, attended, grad_att, stats
    )
    group_span = GROUP // HEAD_DEV
    group_place = tensor_index % group_span
    bit_count = group_span.bit_length() - 1
    running_kv = jnp.stack([key_part, value_part])
    for bit_number in reversed(range(bit_count)):
        half_cols = running_kv.shape[2] // 2
        lower_cols = running_kv[:, :, :half_cols]
        upper_cols = running_kv[:, :, half_cols:]
        upper_half = group_place // (1 << bit_number) % 2 == 1
        kept_cols = jnp.where(upper_half, upper_cols, lower_cols)
        sent_cols = jnp.where(upper_half, lower_cols, upper_cols)
        running_kv = kept_cols + partner(
            sent_cols.astype(jnp.bfloat16), "tensor", bit_number
        ).astype(sent_cols.dtype)
    key_grad = running_kv[0].astype(jnp.bfloat16)
    value_grad = running_kv[1].astype(jnp.bfloat16)
    return (query_grad, key_grad, value_grad, weight_grad)


def solution(mesh):
    torus = Mesh(mesh.devices.reshape(4, 2, mesh.shape["tensor"]), ("dp_0", "dp_1", "tensor"))
    in_specs = (
        P(DP_TENSOR, None),
        P(DP, "tensor"),
        P(DP, "tensor"),
        P(DP, None),
        P(DP, None),
        P(DP, "tensor"),
        P("tensor", DP),
    )
    out_specs = (P(DP, "tensor"), P(DP, "tensor"), P(DP, "tensor"), P(DP, "tensor"))
    return jax.shard_map(
        per_device, mesh=torus, in_specs=in_specs, out_specs=out_specs, check_vma=False
    )
```

profile of v0, /device:TPU:1, one launch (start us, length us, event | category | flops | bytes accessed | tf_op | source)
XLA Modules:
  0.0 373.3 jit_solution(7424440204434012823)
XLA Ops:
  7.2 0.0 copy-start
  7.2 0.0 all-gather.6.cloned.1.call-start
  7.2 0.7 all-gather.6.cloned.1.call-update
  7.9 0.0 all-gather.4.cloned.1.call-start
  8.0 0.7 all-gather.4.cloned.1.call-update
  8.7 0.0 all-gather.8.cloned.1.call-start
  8.7 39.6 %all-gather.6.cloned.1.call-done = bf16[2048,512]{1,0:T(8,128)(2,1)} async-done(((bf16[1024,512]{1,0:T(8,128)(2,1)}), bf16[2048,512]{1,0:T(8,128)(2,1)}) %all-gather.6.cloned.1.call-update) | async-done | bytes 2097168 | tf_op jit(solution)/shard_map/all_gather | solution.py:17
  48.3 0.0 all-gather.8.cloned.1.call-update
  48.3 0.0 copy-start.1
  48.3 0.0 copy-start.2
  48.4 0.0 reduce-scatter.3.cloned.1.call-start
  48.4 112.8 %all-gather.4.cloned.1.call-done = bf16[1024,8192]{1,0:T(8,128)(2,1)} async-done(((bf16[64,8192]{1,0:T(8,128)(2,1)}), bf16[1024,8192]{1,0:T(8,128)(2,1)}) %all-gather.4.cloned.1.call-update) | async-done | bytes 16777232 | tf_op jit(solution)/shard_map/all_gather | solution.py:71
  161.2 14.8 %convolution_convert_fusion = bf16[8192,512]{1,0:T(8,128)(2,1)} fusion(bf16[1024,8192]{1,0:T(8,128)(2,1)} %all-gather.4.cloned.1.call-done, bf16[1024,512]{1,0:T(8,128)(2,1)} %param.12), kind=kOutput, calls=%fused_computation.7 | convolution fusion | flops 8594128896 | bytes 26214400 | tf_op jit(solution)/shard_map/dot_general | solution.py:78
  176.0 0.0 reduce-scatter.3.cloned.1.call-update
  176.0 0.2 reduce-scatter.5.cloned.1.call-start
  176.3 0.0 copy-done.1
  176.3 1.6 copy.26
  177.9 0.0 copy-done.2
  177.9 0.5 copy.27
  178.4 0.3 iota_compare_fusion
  178.7 0.0 copy-start.3
  178.8 0.0 copy-done
  178.8 8.1 %fusion.15 = f32[1024,1024,4]{1,0,2:T(8,128)} fusion(bf16[1024,4,128]{0,2,1:T(8,128)(2,1)S(1)} %bitcast.65, bf16[1024,512]{1,0:T(8,128)(2,1)S(1)} %copy-done, s32[]{:T(128)S(6)} %select_n.56), kind=kOutput, calls=%fused_computation.25 | convolution fusion | flops 1073741824 | bytes 18087940 | tf_op jit(solution)/shard_map/qgd,kd->gqk/dot_general | solution.py:43
  186.9 0.0 copy-start.4
  186.9 56.2 %all-gather.8.cloned.1.call-done = bf16[8192,512]{1,0:T(8,128)(2,1)} async-done(((bf16[2048,512]{1,0:T(8,128)(2,1)}), bf16[8192,512]{1,0:T(8,128)(2,1)}) %all-gather.8.cloned.1.call-update) | async-done | bytes 8388624 | tf_op jit(solution)/shard_map/all_gather | solution.py:17
  243.0 15.6 %multiply_reduce_fusion = (f32[1024,4]{0,1:T(4,128)S(1)}, bf16[1024,512]{0,1:T(8,128)(2,1)}) fusion(f32[1024,512]{0,1:T(8,128)} %copy.26, bf16[1024,8192]{1,0:T(8,128)(2,1)} %all-gather.4.cloned.1.call-done, bf16[8192,512]{1,0:T(8,128)(2,1)} %all-gather.8.cloned.1.call-done), kind=kOutput, calls=%fused_computation.12 | convolution fusion | flops 8592027648 | bytes 28327936 | tf_op jit(solution)/shard_map/dot_general | solution.py:73
  258.6 68.3 %reduce-scatter.3.cloned.1.call-done = bf16[2048,512]{1,0:T(8,128)(2,1)} async-done(((bf16[8192,512]{1,0:T(8,128)(2,1)}), bf16[2048,512]{1,0:T(8,128)(2,1)}) %reduce-scatter.3.cloned.1.call-update) | async-done | bytes 2097168 | tf_op jit(solution)/shard_map/reduce_scatter | solution.py:24
  326.9 0.0 reduce-scatter.5.cloned.1.call-update
  327.0 0.0 copy-done.3
  327.0 0.0 copy-done.4
  327.0 0.0 slice-start
  327.0 0.0 slice-start.1
  327.0 0.0 slice-start.2
  327.0 0.0 copy-start.5
  327.0 11.5 %fusion.1 = bf16[4,1024,1024]{1,2,0:T(8,128)(2,1)} fusion(f32[1024,1024,4]{1,0,2:T(8,128)} %fusion.15, bf16[1024,4,128]{0,2,1:T(8,128)(2,1)} %bitcast.67, f32[4,1024]{1,0:T(4,128)S(1)} %bitcast.69, f32[4,1024]{1,0:T(4,128)S(1)} %copy-done.4, pred[1024,1024]{0,1:T(8,128)(4,1)S(1)} %iota_compare_fusion, bf16[1024,512]{1,0:T(8,128)(2,1)} %param.11, ...), kind=kOutput, calls=%fused_computation.2 | convolution fusion | flops 1098907648 | bytes 27557892 | tf_op jit(solution)/shard_map/qgd,kd->gqk/dot_general | solution.py:48
  338.5 0.0 slice-start.3
  338.5 7.2 %fusion.9 = f32[1,1024,128]{1,2,0:T(8,128)S(1)} fusion(bf16[4,1024,1024]{1,2,0:T(8,128)(2,1)} %fusion.1, bf16[1024,4,128]{0,2,1:T(8,128)(2,1)S(1)} %bitcast.66), kind=kOutput, calls=%fused_computation.16 | convolution fusion | flops 1073872896 | bytes 9961472 | tf_op jit(solution)/shard_map/gqk,qgd->kd/dot_general | solution.py:61
  345.7 0.0 slice-done
  345.7 0.0 slice-done.1
  345.7 0.0 slice-done.2
  345.7 0.0 copy-done.5
  345.7 0.0 slice-done.3
  345.7 5.2 %fusion.10 = f32[1,1024,128]{1,2,0:T(8,128)S(1)} fusion(bf16[1024,4,128]{0,2,1:T(8,128)(2,1)S(1)} %bitcast.68, f32[1024,1024,4]{1,0,2:T(8,128)S(1)} %bitcast.63, f32[4,1024]{1,0:T(4,128)S(1)} %copy-done.4, pred[1024,1024]{0,1:T(8,128)(4,1)} %copy-done.3), kind=kOutput, calls=%fused_computation.17 | convolution fusion | flops 1090519040 | bytes 19415040 | tf_op jit(solution)/shard_map/gqk,qgd->kd/dot_general | solution.py:64
  351.0 0.1 select_convert_fusion
  351.0 1.5 collective-permute-start
  352.5 6.0 %collective-permute-done = bf16[2,1024,64]{1,2,0:T(8,128)(2,1)S(1)} collective-permute-done((bf16[2,1024,64]{1,2,0:T(8,128)(2,1)S(1)}, bf16[2,1024,64]{1,2,0:T(8,128)(2,1)S(1)}, u32[]{:S(2)}, u32[]{:S(2)}) %collective-permute-start) | collective-permute-done | bytes 262176 | tf_op jit(solution)/shard_map/ppermute | solution.py:31
  358.4 0.1 convert_add_fusion
  358.6 1.5 collective-permute-start.1
  360.0 4.7 %multiply_convert_fusion = bf16[128,4,1024]{2,0,1:T(8,128)(2,1)S(1)} fusion(bf16[4,1024,1024]{1,2,0:T(8,128)(2,1)} %fusion.1, bf16[1024,512]{1,0:T(8,128)(2,1)S(1)} %copy-done, s32[]{:T(128)S(6)} %select_n.56), kind=kOutput, calls=%fused_computation.11 | convolution fusion | flops 1074790400 | bytes 9699332 | tf_op jit(solution)/shard_map/gqk,kd->qgd/dot_general | solution.py:56
  364.7 1.3 copy.19
  366.1 0.0 collective-permute-done.1
  366.1 0.7 slice_bitcast_fusion
  366.8 0.0 reduce-scatter.5.cloned.1.call-done
  (3 shorter events, 0.1 us)
Async XLA Ops:
  7.2 171.6 %copy-start = (bf16[1024,512]{1,0:T(8,128)(2,1)S(1)}, bf16[1024,512]{1,0:T(8,128)(2,1)}, u32[]{:S(2)}) copy-start(bf16[1024,512]{1,0:T(8,128)(2,1)} %param.10) | copy-start | bytes 3145732
  7.2 41.1 %all-gather.6.cloned.1.call-start = ((), (), s32[]{:S(2)}) async-start(), calls=%async_computation.3 | async-start | bytes 3145728 | tf_op jit(solution)/shard_map/all_gather | solution.py:17
  7.9 153.3 %all-gather.4.cloned.1.call-start = ((), (), s32[]{:S(2)}) async-start(), calls=%async_computation.2 | async-start | bytes 17825792 | tf_op jit(solution)/shard_map/all_gather | solution.py:71
  8.7 234.3 %all-gather.8.cloned.1.call-start = ((), (), s32[]{:S(2)}) async-start(), calls=%async_computation.4 | async-start | bytes 10485760 | tf_op jit(solution)/shard_map/all_gather | solution.py:17
  48.3 127.9 %copy-start.1 = (bf16[1024,512]{1,0:T(8,128)(2,1)S(1)}, bf16[1024,512]{1,0:T(8,128)(2,1)}, u32[]{:S(2)}) copy-start(bf16[1024,512]{1,0:T(8,128)(2,1)} %param.12) | copy-start | bytes 3145732
  48.3 129.5 %copy-start.2 = (bf16[1024,512]{1,0:T(8,128)(2,1)S(1)}, bf16[1024,512]{1,0:T(8,128)(2,1)}, u32[]{:S(2)}) copy-start(bf16[1024,512]{1,0:T(8,128)(2,1)} %param.9) | copy-start | bytes 3145732
  48.4 278.6 %reduce-scatter.3.cloned.1.call-start = ((), (), s32[]{:S(2)}) async-start(), calls=%async_computation.5 | async-start | bytes 10485760 | tf_op jit(solution)/shard_map/reduce_scatter | solution.py:24
  176.0 190.8 %reduce-scatter.5.cloned.1.call-start = ((), (), s32[]{:S(2)}) async-start(), calls=%async_computation.6 | async-start | bytes 3145728 | tf_op jit(solution)/shard_map/reduce_scatter | solution.py:24
  178.7 148.2 %copy-start.3 = (pred[1024,1024]{0,1:T(8,128)(4,1)}, pred[1024,1024]{0,1:T(8,128)(4,1)S(1)}, u32[]{:S(2)}) copy-start(pred[1024,1024]{0,1:T(8,128)(4,1)S(1)} %iota_compare_fusion) | copy-start | bytes 3145732
  186.9 140.1 %copy-start.4 = (f32[4,1024]{1,0:T(4,128)S(1)}, f32[4,1024]{1,0:T(4,128)}, u32[]{:S(2)}) copy-start(f32[4,1024]{1,0:T(4,128)} %param.13) | copy-start | bytes 49156
  327.0 18.7 %slice-start = ((s8[16777216]{0:T(1024)(128)(4,1)}), s8[4194304]{0:T(1024)(128)(4,1)S(1)}, s32[]{:S(2)}) async-start(s8[16777216]{0:T(1024)(128)(4,1)} %bitcast.62), calls=%async_computation.7 | async-start | bytes 8388608
  327.0 18.7 %slice-start.1 = ((s8[16777216]{0:T(1024)(128)(4,1)}), s8[4194304]{0:T(1024)(128)(4,1)S(1)}, s32[]{:S(2)}) async-start(s8[16777216]{0:T(1024)(128)(4,1)} %bitcast.62), calls=%async_computation.8 | async-start | bytes 8388608
  327.0 18.7 %slice-start.2 = ((s8[16777216]{0:T(1024)(128)(4,1)}), s8[4194304]{0:T(1024)(128)(4,1)S(1)}, s32[]{:S(2)}) async-start(s8[16777216]{0:T(1024)(128)(4,1)} %bitcast.62), calls=%async_computation.9 | async-start | bytes 8388608
  327.0 18.7 %copy-start.5 = (bf16[1024,512]{0,1:T(8,128)(2,1)S(1)}, bf16[1024,512]{0,1:T(8,128)(2,1)}, u32[]{:S(2)}) copy-start(bf16[1024,512]{0,1:T(8,128)(2,1)} %get-tuple-element.11) | copy-start | bytes 3145732
  338.5 7.2 %slice-start.3 = ((s8[16777216]{0:T(1024)(128)(4,1)}), s8[4194304]{0:T(1024)(128)(4,1)S(1)}, s32[]{:S(2)}) async-start(s8[16777216]{0:T(1024)(128)(4,1)} %bitcast.62), calls=%async_computation.10 | async-start | bytes 8388608
  351.0 7.4 %collective-permute-start = (bf16[2,1024,64]{1,2,0:T(8,128)(2,1)S(1)}, bf16[2,1024,64]{1,2,0:T(8,128)(2,1)S(1)}, u32[]{:S(2)}, u32[]{:S(2)}) collective-permute-start(bf16[2,1024,64]{1,2,0:T(8,128)(2,1)S(1)} %select_convert_fusion), channel_id=1, source_target_pairs={{0,2},{1,3},{2,0},{3,1},{4,6},{5,7},{6,4},{7,5},{8,10},{9,11},{10,... | collective-permute-start | bytes 786440 | tf_op jit(solution)/shard_map/ppermute | solution.py:31
  358.6 7.5 %collective-permute-start.1 = (bf16[2,1024,32]{1,2,0:T(8,128)(2,1)S(1)}, bf16[2,1024,32]{1,2,0:T(8,128)(2,1)S(1)}, u32[]{:S(2)}, u32[]{:S(2)}) collective-permute-start(bf16[2,1024,32]{1,2,0:T(8,128)(2,1)S(1)} %select_convert_fusion.1), channel_id=1, source_target_pairs={{0,1},{1,0},{2,3},{3,2},{4,5},{5,4},{6,7},{7,6},{8,9},{9,8},{10,11... | collective-permute-start | bytes 393224 | tf_op jit(solution)/shard_map/ppermute | solution.py:31
Sparse Core Ops, SparseCore 0:
  9.6 38.6 all-gather.5
  50.8 110.3 all-gather.3
  162.9 80.0 all-gather.7
  245.3 81.5 reduce-scatter.2
  329.7 34.0 reduce-scatter.4
where the time goes:
time: 373 us
  waiting for transfers between devices  284 us (76%)
  matrix products  67 us (18%)
  between operations  14 us (4%)
  local copies, waits for them, and re-layouts  4.17 us (1%)
    all_gather x1, waiting for transfers between devices, per_device(): grad_rows = lax.all_gather(grad_out, 'tensor', axis=0, tiled=True)  113 us
    all_gather x2, waiting for transfers between devices, gathered_by_axis(): nearer = lax.all_gather(x, axes[-1], axis=dim, tiled=True)  95.7 us
    reduce_scatter x2, waiting for transfers between devices, sum_by_axis(): subtotal = lax.psum_scatter(subtotal, axis, scatter_dimension=0, tiled=True)  68.3 us
    dot_general x1, matrix products, per_device(): jnp.dot(grad_block, gathered_by_axis(out_weight, DP, 0), preferred_elemen...  15.6 us
    dot_general x1, matrix products, per_device(): lax.dot_general(grad_block, attended, (((0,), (0,)), ((), ())), preferred...  14.8 us
    dot_general x1, matrix products, attention_grads(): jnp.einsum('qgd,kd->gqk', grad_heads, value_one, preferred_element_type=j...  11.5 us
    dot_general x1, matrix products, attention_grads(): jnp.einsum('qgd,kd->gqk', query_heads, key_one, preferred_element_type=jn...  8.09 us
  transfers between devices with their start and end apart: 7, of which 5 were waited for; matrix products, arithmetic and copies ran while one was open for 19% of the time, Pallas kernels for 0%

commit v1 on v0

--- a/solution.py
+++ b/solution.py
@@ -68,7 +68,8 @@
 
 
 def per_device(grad_out, out_weight, query, keys, values, attended, stats):
-    grad_rows = lax.all_gather(grad_out, "tensor", axis=0, tiled=True)
+    sent = jnp.stack([grad_out] * lax.axis_size("tensor"))
+    grad_rows = jnp.concatenate(lax.all_to_all(sent, "tensor", 0, 0), axis=0)
     grad_block = grad_rows
     grad_att = jnp.dot(
         grad_block, gathered_by_axis(out_weight, DP, 0), preferred_element_type=jnp.float32

time: 373 us -> 451 us (1.21)
  waiting for transfers between devices: 284 us -> 342 us
  starting transfers between devices: 3.3 us -> 12.7 us
  local copies, waits for them, and re-layouts: 4.17 us -> 11.1 us
    all_to_all x0 -> x1, waiting for transfers between devices: none -> 201 us  [per_device(): grad_rows = jnp.concatenate(lax.all_to_all(sent, 'tensor', 0, 0), axis=0)]
    all_gather x1 -> x0, waiting for transfers between devices: 113 us -> none  [per_device(): grad_rows = lax.all_gather(grad_out, 'tensor', axis=0, tiled=True)]
    all_gather x2, waiting for transfers between devices: 95.7 us -> 61 us  [gathered_by_axis(): nearer = lax.all_gather(x, axes[-1], axis=dim, tiled=True)]
    all_to_all x0 -> x1, starting transfers between devices: none -> 9.41 us  [per_device(): grad_rows = jnp.concatenate(lax.all_to_all(sent, 'tensor', 0, 0), axis=0)]
    another operation x0 -> x1, local copies, waits for them, and re-layouts: none -> 6.9 us  [per_device(): sent = jnp.stack([grad_out] * lax.axis_size('tensor'))]
    reduce_scatter x2, waiting for transfers between devices: 68.3 us -> 73.7 us  [sum_by_axis(): subtotal = lax.psum_scatter(subtotal, axis, scatter_dimension=0, tiled=True)]
  transfers between devices with their start and end apart: 7 -> 7, of which waited for: 5 -> 4; matrix products, arithmetic and copies ran while one was open for 19% -> 17% of each run, Pallas kernels for 0% -> 0%
where the time goes in v1:
time: 451 us; the launch traced here: 450 us
  waiting for transfers between devices  342 us (76%)
  matrix products  69.8 us (15%)
  between operations  14 us (3%)
  starting transfers between devices  12.7 us (3%)
  local copies, waits for them, and re-layouts  11.1 us (2%)
    all_to_all x1, waiting for transfers between devices, per_device(): grad_rows = jnp.concatenate(lax.all_to_all(sent, 'tensor', 0, 0), axis=0)  201 us
    reduce_scatter x2, waiting for transfers between devices, sum_by_axis(): subtotal = lax.psum_scatter(subtotal, axis, scatter_dimension=0, tiled=True)  73.7 us
    all_gather x2, waiting for transfers between devices, gathered_by_axis(): nearer = lax.all_gather(x, axes[-1], axis=dim, tiled=True)  61 us
    dot_general x1, matrix products, per_device(): lax.dot_general(grad_block, attended, (((0,), (0,)), ((), ())), preferred...  17.5 us
    dot_general x1, matrix products, per_device(): jnp.dot(grad_block, gathered_by_axis(out_weight, DP, 0), preferred_elemen...  15.6 us
    dot_general x1, matrix products, attention_grads(): jnp.einsum('qgd,kd->gqk', grad_heads, value_one, preferred_element_type=j...  11.5 us
    all_to_all x1, starting transfers between devices, per_device(): grad_rows = jnp.concatenate(lax.all_to_all(sent, 'tensor', 0, 0), axis=0)  9.41 us
  transfers between devices with their start and end apart: 7, of which 4 were waited for; matrix products, arithmetic and copies ran while one was open for 17% of the time, Pallas kernels for 0%

profile of v1, /device:TPU:1, one launch (start us, length us, event | category | flops | bytes accessed | tf_op | source)
XLA Modules:
  0.0 450.3 jit_solution(6925256552827773162)
XLA Ops:
  7.2 0.0 copy-start
  7.2 6.9 %stack.8 = bf16[16,64,8192]{2,1,0:T(8,128)(2,1)} broadcast(bf16[64,8192]{1,0:T(8,128)(2,1)} %param.7), dimensions={1,2} | broadcast | bytes 17825792 | tf_op jit(solution)/shard_map/stack | solution.py:71
  14.1 0.0 copy-start.1
  14.1 9.4 %all-to-all-start = ((bf16[16,64,8192]{2,1,0:T(8,128)(2,1)}), bf16[16,64,8192]{2,1,0:T(8,128)(2,1)}, u32[]{:S(2)}, u32[]{:S(2)}) async-start(bf16[16,64,8192]{2,1,0:T(8,128)(2,1)} %stack.8), calls=%async_computation | async-start | bytes 33554432 | tf_op jit(solution)/shard_map/all_to_all | solution.py:72
  23.5 0.0 all-gather.3.cloned.1.call-start
  23.5 0.7 all-gather.3.cloned.1.call-update
  24.2 0.0 all-gather.5.cloned.1.call-start
  24.3 61.0 %all-gather.3.cloned.1.call-done = bf16[2048,512]{1,0:T(8,128)(2,1)} async-done(((bf16[1024,512]{1,0:T(8,128)(2,1)}), bf16[2048,512]{1,0:T(8,128)(2,1)}) %all-gather.3.cloned.1.call-update) | async-done | bytes 2097168 | tf_op jit(solution)/shard_map/all_gather | solution.py:17
  85.3 0.0 all-gather.5.cloned.1.call-update
  85.3 0.0 reduce-scatter.3.cloned.1.call-start
  85.4 200.8 %all-to-all-done = bf16[16,64,8192]{2,1,0:T(8,128)(2,1)} async-done(((bf16[16,64,8192]{2,1,0:T(8,128)(2,1)}), bf16[16,64,8192]{2,1,0:T(8,128)(2,1)}, u32[]{:S(2)}, u32[]{:S(2)}) %all-to-all-start) | async-done | bytes 16777248 | tf_op jit(solution)/shard_map/all_to_all | solution.py:72
  286.2 0.0 copy-done.1
  286.2 0.0 copy-start.2
  286.2 17.5 %convolution_convert_fusion = bf16[8192,512]{1,0:T(8,128)(2,1)} fusion(bf16[1024,8192]{1,0:T(8,128)(2,1)} %bitcast.4, bf16[1024,512]{1,0:T(8,128)(2,1)S(1)} %copy-done.1), kind=kOutput, calls=%fused_computation.7 | convolution fusion | flops 8594128896 | bytes 26214400 | tf_op jit(solution)/shard_map/dot_general | solution.py:79
  303.8 0.0 reduce-scatter.3.cloned.1.call-update
  303.8 0.2 reduce-scatter.5.cloned.1.call-start
  304.0 1.6 copy.26
  305.7 0.0 copy-done.2
  305.7 0.5 copy.27
  306.2 0.3 iota_compare_fusion
  306.5 0.0 copy-start.3
  306.5 0.0 copy-done
  306.6 8.1 %fusion.15 = f32[1024,1024,4]{1,0,2:T(8,128)} fusion(bf16[1024,4,128]{0,2,1:T(8,128)(2,1)S(1)} %bitcast.66, bf16[1024,512]{1,0:T(8,128)(2,1)S(1)} %copy-done, s32[]{:T(128)S(6)} %select_n.56), kind=kOutput, calls=%fused_computation.25 | convolution fusion | flops 1073741824 | bytes 18087940 | tf_op jit(solution)/shard_map/qgd,kd->gqk/dot_general | solution.py:43
  314.6 0.0 copy-start.4
  314.6 0.0 all-gather.5.cloned.1.call-done
  314.6 15.6 %multiply_reduce_fusion = (f32[1024,4]{0,1:T(4,128)S(1)}, bf16[1024,512]{0,1:T(8,128)(2,1)}) fusion(f32[1024,512]{0,1:T(8,128)} %copy.26, bf16[1024,8192]{1,0:T(8,128)(2,1)} %bitcast.4, bf16[8192,512]{1,0:T(8,128)(2,1)} %all-gather.5.cloned.1.call-done), kind=kOutput, calls=%fused_computation.12 | convolution fusion | flops 8592027648 | bytes 28327936 | tf_op jit(solution)/shard_map/dot_general | solution.py:74
  330.2 73.7 %reduce-scatter.3.cloned.1.call-done = bf16[2048,512]{1,0:T(8,128)(2,1)} async-done(((bf16[8192,512]{1,0:T(8,128)(2,1)}), bf16[2048,512]{1,0:T(8,128)(2,1)}) %reduce-scatter.3.cloned.1.call-update) | async-done | bytes 2097168 | tf_op jit(solution)/shard_map/reduce_scatter | solution.py:24
  403.9 0.0 reduce-scatter.5.cloned.1.call-update
  403.9 0.0 copy-done.3
  404.0 0.0 copy-done.4
  404.0 0.0 slice-start
  404.0 0.0 slice-start.1
  404.0 0.0 slice-start.2
  404.0 0.0 copy-start.5
  404.0 11.5 %fusion.1 = bf16[4,1024,1024]{1,2,0:T(8,128)(2,1)} fusion(f32[1024,1024,4]{1,0,2:T(8,128)} %fusion.15, bf16[1024,4,128]{0,2,1:T(8,128)(2,1)} %bitcast.68, f32[4,1024]{1,0:T(4,128)S(1)} %bitcast.70, f32[4,1024]{1,0:T(4,128)S(1)} %copy-done.4, pred[1024,1024]{0,1:T(8,128)(4,1)S(1)} %iota_compare_fusion, bf16[1024,512]{1,0:T(8,128)(2,1)} %param.11, ...), kind=kOutput, calls=%fused_computation.2 | convolution fusion | flops 1098907648 | bytes 27557892 | tf_op jit(solution)/shard_map/qgd,kd->gqk/dot_general | solution.py:48
  415.5 0.0 slice-start.3
  415.5 7.2 %fusion.9 = f32[1,1024,128]{1,2,0:T(8,128)S(1)} fusion(bf16[4,1024,1024]{1,2,0:T(8,128)(2,1)} %fusion.1, bf16[1024,4,128]{0,2,1:T(8,128)(2,1)S(1)} %bitcast.67), kind=kOutput, calls=%fused_computation.16 | convolution fusion | flops 1073872896 | bytes 9961472 | tf_op jit(solution)/shard_map/gqk,qgd->kd/dot_general | solution.py:61
  422.6 0.0 slice-done
  422.6 0.0 slice-done.1
  422.7 0.0 slice-done.2
  422.7 0.0 copy-done.5
  422.7 0.0 slice-done.3
  422.7 5.2 %fusion.10 = f32[1,1024,128]{1,2,0:T(8,128)S(1)} fusion(bf16[1024,4,128]{0,2,1:T(8,128)(2,1)S(1)} %bitcast.69, f32[1024,1024,4]{1,0,2:T(8,128)S(1)} %bitcast.64, f32[4,1024]{1,0:T(4,128)S(1)} %copy-done.4, pred[1024,1024]{0,1:T(8,128)(4,1)} %copy-done.3), kind=kOutput, calls=%fused_computation.17 | convolution fusion | flops 1090519040 | bytes 19415040 | tf_op jit(solution)/shard_map/gqk,qgd->kd/dot_general | solution.py:64
  427.9 0.1 select_convert_fusion
  428.0 1.5 collective-permute-start
  429.5 5.9 %collective-permute-done = bf16[2,1024,64]{1,2,0:T(8,128)(2,1)S(1)} collective-permute-done((bf16[2,1024,64]{1,2,0:T(8,128)(2,1)S(1)}, bf16[2,1024,64]{1,2,0:T(8,128)(2,1)S(1)}, u32[]{:S(2)}, u32[]{:S(2)}) %collective-permute-start) | collective-permute-done | bytes 262176 | tf_op jit(solution)/shard_map/ppermute | solution.py:31
  435.4 0.1 convert_add_fusion
  435.5 1.5 collective-permute-start.1
  437.0 4.7 %multiply_convert_fusion = bf16[128,4,1024]{2,0,1:T(8,128)(2,1)S(1)} fusion(bf16[4,1024,1024]{1,2,0:T(8,128)(2,1)} %fusion.1, bf16[1024,512]{1,0:T(8,128)(2,1)S(1)} %copy-done, s32[]{:T(128)S(6)} %select_n.56), kind=kOutput, calls=%fused_computation.11 | convolution fusion | flops 1074790400 | bytes 9699332 | tf_op jit(solution)/shard_map/gqk,kd->qgd/dot_general | solution.py:56
  441.7 1.3 copy.19
  443.1 0.0 collective-permute-done.1
  443.1 0.7 slice_bitcast_fusion
  443.8 0.0 reduce-scatter.5.cloned.1.call-done
  (3 shorter events, 0.1 us)
Async XLA Ops:
  7.2 299.4 %copy-start = (bf16[1024,512]{1,0:T(8,128)(2,1)S(1)}, bf16[1024,512]{1,0:T(8,128)(2,1)}, u32[]{:S(2)}) copy-start(bf16[1024,512]{1,0:T(8,128)(2,1)} %param.10) | copy-start | bytes 3145732
  14.1 272.2 %copy-start.1 = (bf16[1024,512]{1,0:T(8,128)(2,1)S(1)}, bf16[1024,512]{1,0:T(8,128)(2,1)}, u32[]{:S(2)}) copy-start(bf16[1024,512]{1,0:T(8,128)(2,1)} %param.12) | copy-start | bytes 3145732
  14.1 272.2 %all-to-all-start = ((bf16[16,64,8192]{2,1,0:T(8,128)(2,1)}), bf16[16,64,8192]{2,1,0:T(8,128)(2,1)}, u32[]{:S(2)}, u32[]{:S(2)}) async-start(bf16[16,64,8192]{2,1,0:T(8,128)(2,1)} %stack.8), calls=%async_computation | async-start | bytes 33554432 | tf_op jit(solution)/shard_map/all_to_all | solution.py:72
  23.5 61.8 %all-gather.3.cloned.1.call-start = ((), (), s32[]{:S(2)}) async-start(), calls=%async_computation.3 | async-start | bytes 3145728 | tf_op jit(solution)/shard_map/all_gather | solution.py:17
  24.2 290.4 %all-gather.5.cloned.1.call-start = ((), (), s32[]{:S(2)}) async-start(), calls=%async_computation.4 | async-start | bytes 10485760 | tf_op jit(solution)/shard_map/all_gather | solution.py:17
  85.3 318.6 %reduce-scatter.3.cloned.1.call-start = ((), (), s32[]{:S(2)}) async-start(), calls=%async_computation.5 | async-start | bytes 10485760 | tf_op jit(solution)/shard_map/reduce_scatter | solution.py:24
  286.2 19.4 %copy-start.2 = (bf16[1024,512]{1,0:T(8,128)(2,1)S(1)}, bf16[1024,512]{1,0:T(8,128)(2,1)}, u32[]{:S(2)}) copy-start(bf16[1024,512]{1,0:T(8,128)(2,1)} %param.9) | copy-start | bytes 3145732
  303.8 139.9 %reduce-scatter.5.cloned.1.call-start = ((), (), s32[]{:S(2)}) async-start(), calls=%async_computation.6 | async-start | bytes 3145728 | tf_op jit(solution)/shard_map/reduce_scatter | solution.py:24
  306.5 97.4 %copy-start.3 = (pred[1024,1024]{0,1:T(8,128)(4,1)}, pred[1024,1024]{0,1:T(8,128)(4,1)S(1)}, u32[]{:S(2)}) copy-start(pred[1024,1024]{0,1:T(8,128)(4,1)S(1)} %iota_compare_fusion) | copy-start | bytes 3145732
  314.6 89.3 %copy-start.4 = (f32[4,1024]{1,0:T(4,128)S(1)}, f32[4,1024]{1,0:T(4,128)}, u32[]{:S(2)}) copy-start(f32[4,1024]{1,0:T(4,128)} %param.13) | copy-start | bytes 49156
  404.0 18.7 %slice-start = ((s8[16777216]{0:T(1024)(128)(4,1)}), s8[4194304]{0:T(1024)(128)(4,1)S(1)}, s32[]{:S(2)}) async-start(s8[16777216]{0:T(1024)(128)(4,1)} %bitcast.63), calls=%async_computation.7 | async-start | bytes 8388608
  404.0 18.7 %slice-start.1 = ((s8[16777216]{0:T(1024)(128)(4,1)}), s8[4194304]{0:T(1024)(128)(4,1)S(1)}, s32[]{:S(2)}) async-start(s8[16777216]{0:T(1024)(128)(4,1)} %bitcast.63), calls=%async_computation.8 | async-start | bytes 8388608
  404.0 18.7 %slice-start.2 = ((s8[16777216]{0:T(1024)(128)(4,1)}), s8[4194304]{0:T(1024)(128)(4,1)S(1)}, s32[]{:S(2)}) async-start(s8[16777216]{0:T(1024)(128)(4,1)} %bitcast.63), calls=%async_computation.9 | async-start | bytes 8388608
  404.0 18.7 %copy-start.5 = (bf16[1024,512]{0,1:T(8,128)(2,1)S(1)}, bf16[1024,512]{0,1:T(8,128)(2,1)}, u32[]{:S(2)}) copy-start(bf16[1024,512]{0,1:T(8,128)(2,1)} %get-tuple-element.11) | copy-start | bytes 3145732
  415.5 7.2 %slice-start.3 = ((s8[16777216]{0:T(1024)(128)(4,1)}), s8[4194304]{0:T(1024)(128)(4,1)S(1)}, s32[]{:S(2)}) async-start(s8[16777216]{0:T(1024)(128)(4,1)} %bitcast.63), calls=%async_computation.10 | async-start | bytes 8388608
  428.0 7.4 %collective-permute-start = (bf16[2,1024,64]{1,2,0:T(8,128)(2,1)S(1)}, bf16[2,1024,64]{1,2,0:T(8,128)(2,1)S(1)}, u32[]{:S(2)}, u32[]{:S(2)}) collective-permute-start(bf16[2,1024,64]{1,2,0:T(8,128)(2,1)S(1)} %select_convert_fusion), channel_id=1, source_target_pairs={{0,2},{1,3},{2,0},{3,1},{4,6},{5,7},{6,4},{7,5},{8,10},{9,11},{10,... | collective-permute-start | bytes 786440 | tf_op jit(solution)/shard_map/ppermute | solution.py:31
  435.5 7.5 %collective-permute-start.1 = (bf16[2,1024,32]{1,2,0:T(8,128)(2,1)S(1)}, bf16[2,1024,32]{1,2,0:T(8,128)(2,1)S(1)}, u32[]{:S(2)}, u32[]{:S(2)}) collective-permute-start(bf16[2,1024,32]{1,2,0:T(8,128)(2,1)S(1)} %select_convert_fusion.1), channel_id=1, source_target_pairs={{0,1},{1,0},{2,3},{3,2},{4,5},{5,4},{6,7},{7,6},{8,9},{9,8},{10,11... | collective-permute-start | bytes 393224 | tf_op jit(solution)/shard_map/ppermute | solution.py:31
Sparse Core Ops, SparseCore 0:
  26.0 59.3 all-gather.2
  87.0 83.8 all-gather.4
  303.9 99.9 reduce-scatter.2
  406.7 34.0 reduce-scatter.4
